TPU v7x, 16 devices: a 4x2x1 block of a 4x4x8 slice. The times are simulated.
16 devices in a mesh: rep: 2 (over y, z), dp: 8 (over x, core).
Axes of the slice: x: 4, y: 2, z: 1, core: 2. Of those that a mesh axis runs over, the one named last changes fastest.
The devices are a block of a 4x4x8 slice.
Arguments:
- x: bfloat16 [16, 2048, 1280], P(('rep', 'dp')), parts along dimension 0
- dy: bfloat16 [16, 2048, 1280], P(('rep', 'dp')), parts along dimension 0
- w_gate: bfloat16 [2, 1280, 3584], replicated
- w_up: bfloat16 [2, 1280, 3584], replicated
- w_down: bfloat16 [2, 3584, 1280], replicated
- m_w_gate: float32 [2, 1280, 3584], P(None, 'dp')
- m_w_up: float32 [2, 1280, 3584], P(None, 'dp')
- m_w_down: float32 [2, 3584, 1280], P(None, 'dp')
- v_w_gate: float32 [2, 1280, 3584], P(None, 'dp')
- v_w_up: float32 [2, 1280, 3584], P(None, 'dp')
- v_w_down: float32 [2, 3584, 1280], P(None, 'dp')
Outputs:
- output 1: bfloat16 [4, 1280, 3584], P('rep'), parts along dimension 0
- output 2: bfloat16 [4, 1280, 3584], P('rep'), parts along dimension 0
- output 3: bfloat16 [4, 3584, 1280], P('rep'), parts along dimension 0
- output 4: float32 [4, 1280, 3584], P('rep', 'dp'), parts along dimension 0
- output 5: float32 [4, 1280, 3584], P('rep', 'dp'), parts along dimension 0
- output 6: float32 [4, 3584, 1280], P('rep', 'dp'), parts along dimension 0
- output 7: float32 [4, 1280, 3584], P('rep', 'dp'), parts along dimension 0
- output 8: float32 [4, 1280, 3584], P('rep', 'dp'), parts along dimension 0
- output 9: float32 [4, 3584, 1280], P('rep', 'dp'), parts along dimension 0
There are 2 independent parts. A program takes and returns all parts, laid end to end along the dimension named above; an argument that names none is the same for every part.
All inputs are finite; a program needn't handle non-finite values.
Results may differ from a plain program's by a relative error of at most 0.02.
Values are sent between devices in bfloat16 or wider.
A program may use at most 768 MiB of HBM per device.

v0:
```python
import jax
import jax.numpy as jnp
from jax import lax

NAMES = ("w_gate", "w_up", "w_down")


def matmul(a, w):
    return jnp.dot(a, w, preferred_element_type=jnp.float32).astype(jnp.bfloat16)


def normed(h):
    wide = h.astype(jnp.float32)
    scale = lax.rsqrt(jnp.mean(wide**2, -1, keepdims=True) + 1e-6)
    return (wide * scale).astype(jnp.bfloat16)


def layer(h, w):
    a = normed(h)
    gate = jnp.dot(a, w["w_gate"], preferred_element_type=jnp.float32)
    up = jnp.dot(a, w["w_up"], preferred_element_type=jnp.float32)
    return h + matmul((jax.nn.silu(gate) * up).astype(jnp.bfloat16), w["w_down"])


def adamw(w, m, v, g):
    m = 0.9 * m + 0.1 * g
    v = 0.95 * v + 0.05 * g * g
    step = m * lax.rsqrt(v + 1e-8) + 0.1 * w
    return (w - 0.02 * step).astype(jnp.bfloat16), m, v


def stack(weights, h):
    for number in range(weights["w_gate"].shape[0]):
        h = layer(h, {name: w[number] for name, w in weights.items()})
    return h


def solution(mesh):
    groups = mesh.shape["rep"]

    def step(x, dy, *arrays):
        weights, m, v = (arrays[i : i + 3] for i in (0, 3, 6))
        x, dy = (t.reshape(groups, -1, *t.shape[1:]) for t in (x, dy))

        def of_a_group(x, dy):
            _, back = jax.vjp(lambda w: stack(w, x), dict(zip(NAMES, weights, strict=True)))
            by_weights = back(dy)[0]
            gradients = [by_weights[name].astype(jnp.float32) for name in NAMES]
            new = [adamw(w.astype(jnp.float32), m, v, g) for w, m, v, g in zip(weights, m, v, gradients, strict=True)]
            return tuple(one[which] for which in range(3) for one in new)

        return tuple(t.reshape(-1, *t.shape[2:]) for t in jax.vmap(of_a_group)(x, dy))

    return step
```

profile of v0, /device:TPU:113, one launch (start us, length us, event | category | flops | bytes accessed | tf_op | source)
XLA Modules:
  0.0 1170.9 jit_solution(1089504044351558107)
XLA Ops:
  18.9 27.2 %fusion.63 = f32[2048,3584]{1,0:T(8,128)} fusion(bf16[2,1280,3584]{2,1,0:T(8,128)(2,1)} %param, bf16[1,2048,1280]{2,1,0:T(8,128)(2,1)} %param.2, f32[2048]{0:T(1024)S(1)} %add_rsqrt_fusion), kind=kOutput, calls=%fused_computation.78 | convolution fusion | flops 18798346240 | bytes 43786240 | tf_op jit(solution)/vmap(jvp())/dot_general | solution.py:20
  46.1 25.3 %fusion.61 = f32[2048,3584]{1,0:T(8,128)} fusion(bf16[2,1280,3584]{2,1,0:T(8,128)(2,1)} %param.3, bf16[1,2048,1280]{2,1,0:T(8,128)(2,1)S(1)} %bitcast.331, f32[2048]{0:T(1024)S(1)} %add_rsqrt_fusion), kind=kOutput, calls=%fused_computation.76 | convolution fusion | flops 18798346240 | bytes 43786240 | tf_op jit(solution)/vmap(jvp())/dot_general | solution.py:21
  71.4 25.8 %fusion.35 = bf16[2048,3584]{1,0:T(8,128)(2,1)} fusion(f32[2048,3584]{1,0:T(8,128)} %fusion.61, f32[2048,3584]{1,0:T(8,128)} %fusion.63), kind=kLoop, calls=%fused_computation.47 | loop fusion | flops 44040192 | bytes 73400320
  97.2 27.1 %fusion.47 = (f32[2048]{0:T(1024)S(1)}, bf16[1,1,2048,1280]{2,3,1,0:T(8,128)(2,1)}) fusion(bf16[2048,3584]{1,0:T(8,128)(2,1)} %fusion.35, bf16[2,3584,1280]{2,1,0:T(8,128)(2,1)} %param.4, bf16[1,2048,1280]{1,2,0:T(8,128)(2,1)} %copy), kind=kOutput, calls=%fused_computation.61 | convolution fusion | flops 18803587072 | bytes 34349056 | tf_op jit(solution)/vmap(jvp())/dot_general | solution.py:9
  124.9 27.1 %fusion.50 = f32[2048,3584]{1,0:T(8,128)} fusion(bf16[2,1280,3584]{2,1,0:T(8,128)(2,1)} %param, bf16[1,1,2048,1280]{2,3,1,0:T(8,128)(2,1)} %get-tuple-element.10, f32[2048]{0:T(1024)S(1)} %bitcast.342), kind=kOutput, calls=%fused_computation.65 | convolution fusion | flops 18798346240 | bytes 43786240 | tf_op jit(solution)/vmap(jvp())/dot_general | solution.py:20
  152.0 25.9 %fusion.54 = f32[2048,3584]{1,0:T(8,128)} fusion(bf16[2,1280,3584]{2,1,0:T(8,128)(2,1)} %param.3, bf16[1,1,2048,1280]{2,3,1,0:T(8,128)(2,1)S(1)} %copy-done.1, f32[2048]{0:T(1024)S(1)} %bitcast.343), kind=kOutput, calls=%fused_computation.69 | convolution fusion | flops 18798346240 | bytes 43786240 | tf_op jit(solution)/vmap(jvp())/dot_general | solution.py:21
  177.8 31.6 %convolution_bitcast_fusion.1 = f32[1,3584,1280]{2,1,0:T(8,128)} fusion(f32[2048,3584]{1,0:T(8,128)} %fusion.54, f32[2048,3584]{1,0:T(8,128)} %fusion.50, bf16[1,2048,1280]{2,1,0:T(8,128)(2,1)S(1)} %bitcast.338), kind=kOutput, calls=%fused_computation.43 | convolution fusion | flops 18834522112 | bytes 82313216 | tf_op jit(solution)/vmap(transpose(jvp()))/dot_general | solution.py:9
  217.7 26.1 %convolution_convert_fusion.1 = bf16[2048,3584]{1,0:T(8,128)(2,1)} fusion(bf16[2,3584,1280]{2,1,0:T(8,128)(2,1)} %param.4, bf16[1,2048,1280]{2,1,0:T(8,128)(2,1)} %param.5), kind=kOutput, calls=%fused_computation.46 | convolution fusion | flops 18797821952 | bytes 29097984 | tf_op jit(solution)/vmap(transpose(jvp()))/dot_general | solution.py:9
  243.7 30.1 %fusion.6 = bf16[2048,3584]{1,0:T(8,128)(2,1)} fusion(f32[2048,3584]{1,0:T(8,128)} %fusion.50, f32[2048,3584]{1,0:T(8,128)} %fusion.54, bf16[2048,3584]{1,0:T(8,128)(2,1)} %convolution_convert_fusion.1), kind=kLoop, calls=%fused_computation.11 | loop fusion | flops 88080384 | bytes 88080384
  273.8 28.1 %fusion.80 = bf16[2048,1280]{0,1:T(8,128)(2,1)} fusion(bf16[2,1280,3584]{2,1,0:T(8,128)(2,1)} %param.3, bf16[2048,3584]{1,0:T(8,128)(2,1)} %convolution_convert_fusion.1, f32[2048,3584]{1,0:T(8,128)} %fusion.50), kind=kOutput, calls=%fused_computation.91 | convolution fusion | flops 18837143552 | bytes 58458112 | tf_op jit(solution)/vmap(transpose(jvp()))/dot_general | solution.py:21
  301.9 27.9 %fusion.49 = (f32[2048]{0:T(1024)S(1)}, bf16[1,1,2048,1280]{2,3,1,0:T(8,128)(2,1)}) fusion(bf16[1,1,2048,1280]{2,3,1,0:T(8,128)(2,1)} %get-tuple-element.10, bf16[2048,1280]{0,1:T(8,128)(2,1)} %fusion.80, bf16[2048,3584]{1,0:T(8,128)(2,1)} %fusion.6, bf16[2,1280,3584]{2,1,0:T(8,128)(2,1)} %param), kind=kOutput, calls=%fused_computation.63 | convolution fusion | flops 18803587072 | bytes 39591936 | tf_op jit(solution)/vmap(transpose(jvp()))/dot_general | solution.py:20
  342.2 25.5 %convolution_bitcast_fusion = f32[1,3584,1280]{2,1,0:T(8,128)} fusion(bf16[2048,3584]{1,0:T(8,128)(2,1)} %fusion.35, bf16[2048,1280]{0,1:T(8,128)(2,1)} %fusion.100), kind=kOutput, calls=%fused_computation.42 | convolution fusion | flops 18790481920 | bytes 38273024 | tf_op jit(solution)/vmap(transpose(jvp()))/dot_general | solution.py:9
  367.9 28.1 %convolution_bitcast_fusion.2 = f32[1,1280,3584]{2,1,0:T(8,128)} fusion(bf16[2048,3584]{1,0:T(8,128)(2,1)} %fusion.6, bf16[1,1,2048,1280]{2,3,1,0:T(8,128)(2,1)} %get-tuple-element.10, f32[2048]{0:T(1024)S(1)} %bitcast.345), kind=kOutput, calls=%fused_computation.44 | convolution fusion | flops 18798346240 | bytes 38281216 | tf_op jit(solution)/vmap(transpose(jvp()))/dot_general | solution.py:20
  396.1 25.9 %convolution_convert_fusion = bf16[2048,3584]{1,0:T(8,128)(2,1)} fusion(bf16[2048,1280]{0,1:T(8,128)(2,1)} %fusion.100, bf16[2,3584,1280]{2,1,0:T(8,128)(2,1)} %param.4), kind=kOutput, calls=%fused_computation.45 | convolution fusion | flops 18797821952 | bytes 29097984 | tf_op jit(solution)/vmap(transpose(jvp()))/dot_general | solution.py:9
  422.0 39.0 %fusion.29 = f32[1,1280,3584]{2,1,0:T(8,128)} fusion(f32[2048,3584]{1,0:T(8,128)} %fusion.63, f32[2048,3584]{1,0:T(8,128)} %fusion.61, bf16[2048,3584]{1,0:T(8,128)(2,1)} %convolution_convert_fusion, bf16[1,2048,1280]{1,2,0:T(8,128)(2,1)} %copy, f32[2048]{0:T(1024)S(1)} %copy-done.7), kind=kOutput, calls=%fused_computation.40 | convolution fusion | flops 18879086592 | bytes 97001472 | tf_op jit(solution)/vmap(transpose(jvp()))/dot_general | solution.py:20
  461.2 31.3 %fusion.26 = f32[1,1280,3584]{2,1,0:T(8,128)} fusion(bf16[2048,3584]{1,0:T(8,128)(2,1)} %convolution_convert_fusion.1, f32[2048,3584]{1,0:T(8,128)} %fusion.50, bf16[1,1,2048,1280]{2,3,1,0:T(8,128)(2,1)} %get-tuple-element.10, f32[2048]{0:T(1024)S(1)} %bitcast.346), kind=kOutput, calls=%fused_computation.39 | convolution fusion | flops 18842386432 | bytes 67641344 | tf_op jit(solution)/vmap(transpose(jvp()))/dot_general | solution.py:21
  492.6 31.0 %fusion.32 = f32[1,1280,3584]{2,1,0:T(8,128)} fusion(bf16[2048,3584]{1,0:T(8,128)(2,1)} %convolution_convert_fusion, f32[2048,3584]{1,0:T(8,128)} %fusion.63, bf16[1,2048,1280]{1,2,0:T(8,128)(2,1)} %copy, f32[2048]{0:T(1024)S(1)} %copy-done.7), kind=kOutput, calls=%fused_computation.41 | convolution fusion | flops 18842386432 | bytes 67641344 | tf_op jit(solution)/vmap(transpose(jvp()))/dot_general | solution.py:21
  537.7 25.8 %reduce-scatter.19.cloned.1.call-done = f32[1,160,3584]{2,1,0:T(8,128)} async-done(((f32[1,1280,3584]{2,1,0:T(8,128)}), f32[1,160,3584]{2,1,0:T(8,128)}) %reduce-scatter.19.cloned.1.call-update) | async-done | bytes 2293776
  565.2 95.9 %reduce-scatter.21.cloned.1.call-done = f32[1,160,3584]{2,1,0:T(8,128)} async-done(((f32[1,1280,3584]{2,1,0:T(8,128)}), f32[1,160,3584]{2,1,0:T(8,128)}) %reduce-scatter.21.cloned.1.call-update) | async-done | bytes 2293776
  671.2 87.0 %reduce-scatter.23.cloned.1.call-done = f32[1,160,3584]{2,1,0:T(8,128)} async-done(((f32[1,1280,3584]{2,1,0:T(8,128)}), f32[1,160,3584]{2,1,0:T(8,128)}) %reduce-scatter.23.cloned.1.call-update) | async-done | bytes 2293776
  759.9 95.9 %reduce-scatter.25.cloned.1.call-done = f32[1,160,3584]{2,1,0:T(8,128)} async-done(((f32[1,1280,3584]{2,1,0:T(8,128)}), f32[1,160,3584]{2,1,0:T(8,128)}) %reduce-scatter.25.cloned.1.call-update) | async-done | bytes 2293776
  865.9 79.8 %all-gather.14.cloned.1.call-done = bf16[1,2,3584,1280]{3,2,1,0:T(8,128)(2,1)} async-done(((bf16[1,2,448,1280]{3,2,1,0:T(8,128)(2,1)}), bf16[1,2,3584,1280]{3,2,1,0:T(8,128)(2,1)}) %all-gather.14.cloned.1.call-update) | async-done | bytes 18350096 | tf_op jit(solution)/reshape | solution.py:52
  945.7 90.6 %all-gather.10.cloned.1.call-done = bf16[1,2,1280,3584]{3,2,1,0:T(8,128)(2,1)} async-done(((bf16[1,2,160,3584]{3,2,1,0:T(8,128)(2,1)}), bf16[1,2,1280,3584]{3,2,1,0:T(8,128)(2,1)}) %all-gather.10.cloned.1.call-update) | async-done | bytes 18350096 | tf_op jit(solution)/reshape | solution.py:52
  1036.3 90.6 %all-gather.12.cloned.1.call-done = bf16[1,2,1280,3584]{3,2,1,0:T(8,128)(2,1)} async-done(((bf16[1,2,160,3584]{3,2,1,0:T(8,128)(2,1)}), bf16[1,2,1280,3584]{3,2,1,0:T(8,128)(2,1)}) %all-gather.12.cloned.1.call-update) | async-done | bytes 18350096 | tf_op jit(solution)/reshape | solution.py:52
  (80 shorter events, 107.5 us)
Async XLA Ops:
  7.2 518.3 %reduce-scatter.27.cloned.1.call-start = ((), (), s32[]{:S(2)}) async-start(), calls=%async_computation.13 | async-start | bytes 20643840
  10.8 35.3 %slice-start = ((s8[5242880]{0:T(1024)(128)(4,1)}), s8[1048576]{0:T(1024)(128)(4,1)S(1)}, s32[]{:S(2)}) async-start(s8[5242880]{0:T(1024)(128)(4,1)} %bitcast.330), calls=%async_computation.15 | async-start | bytes 2097152
  18.8 27.3 %copy-start.6 = (f32[2048]{0:T(1024)}, f32[2048]{0:T(1024)S(1)}, u32[]{:S(2)}) copy-start(f32[2048]{0:T(1024)S(1)} %add_rsqrt_fusion) | copy-start | bytes 24580
  18.8 27.3 %slice-start.1 = ((s8[5242880]{0:T(1024)(128)(4,1)}), s8[4194304]{0:T(1024)(128)(4,1)S(1)}, s32[]{:S(2)}) async-start(s8[5242880]{0:T(1024)(128)(4,1)} %bitcast.330), calls=%async_computation.16 | async-start | bytes 8388608
  124.3 27.7 %copy-start.4 = (f32[1,1,2048]{2,1,0:T(1,128)}, f32[1,1,2048]{2,1,0:T(1,128)S(1)}, u32[]{:S(2)}) copy-start(f32[1,1,2048]{2,1,0:T(1,128)S(1)} %rsqrt.31) | copy-start | bytes 24580
  124.9 27.1 %copy-start.1 = (bf16[1,1,2048,1280]{2,3,1,0:T(8,128)(2,1)S(1)}, bf16[1,1,2048,1280]{2,3,1,0:T(8,128)(2,1)}, u32[]{:S(2)}) copy-start(bf16[1,1,2048,1280]{2,3,1,0:T(8,128)(2,1)} %get-tuple-element.10) | copy-start | bytes 15728644
  124.9 53.0 %slice-start.7 = ((s8[5242880]{0:T(1024)(128)(4,1)}), s8[4194304]{0:T(1024)(128)(4,1)S(1)}, s32[]{:S(2)}) async-start(s8[5242880]{0:T(1024)(128)(4,1)} %bitcast.337), calls=%async_computation.22 | async-start | bytes 8388608
  152.0 25.9 %slice-start.8 = ((s8[5242880]{0:T(1024)(128)(4,1)}), s8[1048576]{0:T(1024)(128)(4,1)S(1)}, s32[]{:S(2)}) async-start(s8[5242880]{0:T(1024)(128)(4,1)} %bitcast.337), calls=%async_computation.23 | async-start | bytes 2097152
  209.5 317.8 %reduce-scatter.29.cloned.1.call-start = ((), (), s32[]{:S(2)}) async-start(), calls=%async_computation.14 | async-start | bytes 20643840
  301.9 27.9 %copy-start.3 = (f32[2048]{0:T(1024)S(1)}, f32[2048]{0:T(1024)}, u32[]{:S(2)}) copy-start(f32[2048]{0:T(1024)} %copy-done.2) | copy-start | bytes 24580
  301.9 27.9 %copy-start.5 = (f32[1,1,2048]{2,1,0:T(1,128)S(1)}, f32[1,1,2048]{2,1,0:T(1,128)}, u32[]{:S(2)}) copy-start(f32[1,1,2048]{2,1,0:T(1,128)} %copy-done.4) | copy-start | bytes 24580
  367.8 195.6 %reduce-scatter.19.cloned.1.call-start = ((), (), s32[]{:S(2)}) async-start(), calls=%async_computation.9 | async-start | bytes 20643840
  396.0 26.0 %copy-start.7 = (f32[2048]{0:T(1024)S(1)}, f32[2048]{0:T(1024)}, u32[]{:S(2)}) copy-start(f32[2048]{0:T(1024)} %copy-done.6) | copy-start | bytes 24580
  396.0 265.1 %reduce-scatter.21.cloned.1.call-start = ((), (), s32[]{:S(2)}) async-start(), calls=%async_computation.10 | async-start | bytes 20643840
  461.1 297.0 %reduce-scatter.23.cloned.1.call-start = ((), (), s32[]{:S(2)}) async-start(), calls=%async_computation.11 | async-start | bytes 20643840
  492.5 363.3 %reduce-scatter.25.cloned.1.call-start = ((), (), s32[]{:S(2)}) async-start(), calls=%async_computation.12 | async-start | bytes 20643840
  523.6 422.1 %all-gather.14.cloned.1.call-start = ((), (), s32[]{:S(2)}) async-start(), calls=%async_computation.8 | async-start | bytes 20643840 | tf_op jit(solution)/reshape | solution.py:52
  537.6 498.7 %all-gather.10.cloned.1.call-start = ((), (), s32[]{:S(2)}) async-start(), calls=%async_computation.6 | async-start | bytes 20643840 | tf_op jit(solution)/reshape | solution.py:52
  671.1 455.7 %all-gather.12.cloned.1.call-start = ((), (), s32[]{:S(2)}) async-start(), calls=%async_computation.7 | async-start | bytes 20643840 | tf_op jit(solution)/reshape | solution.py:52
  1126.8 19.7 %copy-start = (bf16[1,2,1280,3584]{3,2,1,0:T(8,128)(2,1)S(1)}, bf16[1,2,1280,3584]{3,2,1,0:T(8,128)(2,1)}, u32[]{:S(2)}) copy-start(bf16[1,2,1280,3584]{3,2,1,0:T(8,128)(2,1)} %all-gather.12.cloned.1.call-done) | copy-start | bytes 55050244
  1126.8 29.0 %slice-start.2 = ((s8[18350080]{0:T(1024)(128)(4,1)}), s8[4194304]{0:T(1024)(128)(4,1)S(1)}, s32[]{:S(2)}) async-start(s8[18350080]{0:T(1024)(128)(4,1)} %bitcast.332), calls=%async_computation.17 | async-start | bytes 8388608
  1126.8 29.0 %slice-start.3 = ((s8[18350080]{0:T(1024)(128)(4,1)}), s8[4194304]{0:T(1024)(128)(4,1)S(1)}, s32[]{:S(2)}) async-start(s8[18350080]{0:T(1024)(128)(4,1)} %bitcast.332), calls=%async_computation.18 | async-start | bytes 8388608
  1126.8 29.0 %slice-start.4 = ((s8[18350080]{0:T(1024)(128)(4,1)}), s8[4194304]{0:T(1024)(128)(4,1)S(1)}, s32[]{:S(2)}) async-start(s8[18350080]{0:T(1024)(128)(4,1)} %bitcast.332), calls=%async_computation.19 | async-start | bytes 8388608
  1146.5 10.7 slice-start.6
  (3 other events, 11.0 us)
Sparse Core Ops, SparseCore 0:
  209.6 97.6 reduce-scatter.26
  367.9 97.6 reduce-scatter.28
  468.5 94.8 reduce-scatter.18
  566.2 94.8 reduce-scatter.20
  663.3 94.8 reduce-scatter.22
  761.0 94.8 reduce-scatter.24
  857.4 88.2 all-gather.13
  947.9 88.3 all-gather.9
  1038.4 88.3 all-gather.11
where the time goes:
time: 1180 us; the launch traced here: 1170 us
  waiting for transfers between devices  566 us (48%)
  matrix products  427 us (36%)
  other arithmetic  107 us (9%)
  local copies, waits for them, and re-layouts  54.9 us (5%)
  between operations  15.1 us (1%)
    unnamed x15, waiting for transfers between devices  305 us
    reshape x3, waiting for transfers between devices, step(): t.reshape(-1, *t.shape[2:])  261 us
    dot_general x5, matrix products, layer(): gate = jnp.dot(a, w['w_gate'], preferred_element_type=jnp.float32)  149 us
    dot_general x5, matrix products, layer(): up = jnp.dot(a, w['w_up'], preferred_element_type=jnp.float32)  141 us
    dot_general x5, matrix products, matmul(): jnp.dot(a, w, preferred_element_type=jnp.float32).astype(jnp.bfloat16)  136 us
    unnamed x6, other arithmetic  68.3 us
    unnamed x41, local copies, waits for them, and re-layouts  54.3 us
    reshape x3, other arithmetic, step(): t.reshape(-1, *t.shape[2:])  24.9 us
  transfers between devices with their start and end apart: 9, of which 7 were waited for; matrix products, arithmetic and copies ran while one was open for 30% of the time, Pallas kernels for 0%

commit v1 on v0

v1 whole, which is shorter than its diff:
```python
import jax
import jax.numpy as jnp
from jax import lax
from jax.experimental import pallas as pl
from jax.experimental.pallas import tpu as pltpu
from jax.sharding import PartitionSpec as P

MESH = pl.DeviceIdType.MESH
STRIP = 16


def adamw(w, m, v, g):
    m = 0.9 * m + 0.1 * g
    v = 0.95 * v + 0.05 * g * g
    step = m * lax.rsqrt(v + 1e-8) + 0.1 * w
    return (w - 0.02 * step).astype(jnp.bfloat16), m, v


def strips(rows, body):
    def one(i, _):
        body(pl.ds(pl.multiple_of(i * STRIP, STRIP), STRIP))
        return ()

    lax.fori_loop(0, rows // STRIP, one, ())


class Unit:
    def __init__(self, number, place, refs, layer, cols, buf, sems):
        self.u, self.p, self.layer, self.cols, self.buf, self.sems = number, place, layer, cols, buf, sems
        self.grad, self.w, self.m, self.v, self.out, self.g = refs
        self.r = self.m.shape[1]
        self.h = self.r // 2

    def slot(self, name):
        return self.buf[name].at[self.u % self.buf[name].shape[0]]

    def sem(self, name, k=None):
        ref = self.sems[name].at[self.u % self.sems[name].shape[0]]
        return ref if k is None else ref.at[k]

    def rows(self, ref, block, half=None):
        start, size = block * self.r, self.r
        if half is not None:
            start, size = start + half * self.h, self.h
        return ref.at[pl.ds(pl.multiple_of(start, STRIP), size), self.cols]

    def remote(self, src, dst, send, recv, to):
        return pltpu.make_async_remote_copy(src_ref=src, dst_ref=dst, send_sem=send, recv_sem=recv, device_id={"dp": to}, device_id_type=MESH)

    def swap(self, k):
        p = self.p
        src = self.rows(self.grad, p.chip(k) * 2 + 1 - p.core)
        return self.remote(src, self.slot("partner").at[k], self.sem("swap_s", k), self.sem("swap_r", k), p.partner)

    def load(self, k):
        return pltpu.make_async_copy(self.rows(self.grad, self.p.chip(k) * 2 + self.p.core), self.slot("mine").at[k], self.sem("load", k))

    def first(self, side, kind):
        half = (side if kind == 0 else 1 - side) * self.h
        k = 1 if kind == 0 else (0 if side == 0 else 2)
        src = self.slot("sums").at[k, pl.ds(half, self.h)]
        i = side * 2 + kind
        return self.remote(src, self.slot("first").at[i], self.sem("first_s", i), self.sem("first_r", i), self.p.side(side))

    def second(self, side):
        src = self.slot("sums").at[0 if side == 0 else 2, pl.ds(side * self.h, self.h)]
        return self.remote(src, self.slot("second").at[side], self.sem("second_s", side), self.sem("second_r", side), self.p.side(side))

    def state(self, i):
        src = (self.m.at[self.layer, :, self.cols], self.v.at[self.layer, :, self.cols])[i] if i < 2 else self.w.at[
            self.layer, pl.ds(pl.multiple_of(self.p.me * self.r, STRIP), self.r), self.cols
        ]
        return pltpu.make_async_copy(src, self.slot(("m", "v", "w")[i]), self.sem("state", i))

    def put(self, i):
        if i == 0:
            return pltpu.make_async_copy(self.slot("new"), self.rows(self.out, self.p.me), self.sem("put", 0))
        return pltpu.make_async_copy(self.slot("g"), self.g.at[:, self.cols], self.sem("put", 1))

    def spread(self, i):
        to = self.p.partner if i == 2 else self.p.side(i)
        return self.remote(self.slot("new"), self.rows(self.out, self.p.me), self.sem("spread_s", i), self.sem("spread_r", i), to)

    def relay(self, side):
        ref = self.rows(self.out, self.p.chip(3 if side == 0 else 1) * 2 + self.p.core, side)
        return self.remote(ref, ref, self.sem("relay_s", side), self.sem("relay_r", side), self.p.side(side))

    def share(self, i):
        ref = self.rows(self.out, self.p.chip((3, 1, 2)[i]) * 2 + self.p.core)
        return self.remote(ref, ref, self.sem("share_s", i), self.sem("share_r", i), self.p.partner)

    def s0(self):
        for k in (2, 1, 3, 0):
            self.swap(k).start()
        for k in (2, 1, 3, 0):
            self.load(k).start()

    def s1(self):
        mine, partner, sums = self.slot("mine"), self.slot("partner"), self.slot("sums")
        for k in (2, 1, 3):
            self.load(k).wait()
            self.swap(k).wait_recv()

            def add(rows, k=k):
                sums[k - 1, rows] = (mine[k, rows].astype(jnp.float32) + partner[k, rows].astype(jnp.float32)).astype(jnp.bfloat16)

            strips(self.r, add)
            if k == 2:
                for side in range(2):
                    self.first(side, 0).start()
            else:
                self.first(0 if k == 1 else 1, 1).start()
        for i in range(3):
            self.state(i).start()

    def s2(self):
        sums, first = self.slot("sums"), self.slot("first")
        for side in range(2):
            self.first(side, 0).wait_recv()
            k, start = 0 if side == 0 else 2, side * self.h

            def add(i, _, side=side, k=k, start=start):
                here = pl.ds(pl.multiple_of(start + i * STRIP, STRIP), STRIP)
                there = pl.ds(pl.multiple_of(i * STRIP, STRIP), STRIP)
                sums[k, here] = (sums[k, here].astype(jnp.float32) + first[side * 2, there].astype(jnp.float32)).astype(jnp.bfloat16)
                return ()

            lax.fori_loop(0, self.h // STRIP, add, ())
            self.second(side).start()

    def s3(self):
        mine, partner, first, second = (self.slot(name) for name in ("mine", "partner", "first", "second"))
        m, v, w, g, new = (self.slot(name) for name in ("m", "v", "w", "g", "new"))
        self.load(0).wait()
        self.swap(0).wait_recv()
        for i in range(3):
            self.state(i).wait()
        for side in range(2):
            self.first(side, 1).wait_recv()
            self.second(side).wait_recv()
        for side in range(2):
            def step(i, _, side=side):
                here = pl.ds(pl.multiple_of(side * self.h + i * STRIP, STRIP), STRIP)
                there = pl.ds(pl.multiple_of(i * STRIP, STRIP), STRIP)
                total = mine[0, here].astype(jnp.float32) + partner[0, here].astype(jnp.float32)
                total = total + second[side, there].astype(jnp.float32) + first[(1 - side) * 2 + 1, there].astype(jnp.float32)
                rounded = total.astype(jnp.bfloat16)
                g[here] = rounded
                new[here] = adamw(w[here].astype(jnp.float32), m[here], v[here], rounded.astype(jnp.float32))[0]
                return ()

            lax.fori_loop(0, self.h // STRIP, step, ())
        for i in range(3):
            self.spread(i).start()
        for i in range(2):
            self.put(i).start()
        for k in range(4):
            self.swap(k).wait_send()
        for i in range(4):
            self.first(i // 2, i % 2).wait_send()
        for side in range(2):
            self.second(side).wait_send()

    def s4(self):
        for side in range(2):
            self.spread(side).wait_recv()
            self.relay(side).start()
            self.share(side).start()
        self.spread(2).wait_recv()
        for i in range(3):
            self.spread(i).wait_send()
        for i in range(2):
            self.put(i).wait()

    def s5(self):
        for side in range(2):
            self.relay(side).wait_recv()
        self.share(2).start()
        for side in range(2):
            self.relay(side).wait_send()
            self.share(side).wait()

    def s6(self):
        self.share(2).wait()


class Place:
    def __init__(self, size):
        assert size == 8
        self.me = lax.axis_index("dp")
        self.core = lax.rem(self.me, 2)
        self.at = self.me // 2
        self.partner = self.me + 1 - 2 * self.core

    def chip(self, k):
        return lax.rem(self.at + k, 4)

    def side(self, side):
        return self.chip(1 if side == 0 else 3) * 2 + self.core


RING = {"mine": 4, "partner": 4, "sums": 3, "first": 3, "second": 3, "m": 3, "v": 3, "w": 3, "g": 3, "new": 3}
SEMS = {"swap_s": 4, "swap_r": 4, "load": 4, "first_s": 4, "first_r": 4, "second_s": 2, "second_r": 2, "state": 3, "put": 2,
        "spread_s": 3, "spread_r": 3, "relay_s": 2, "relay_r": 2, "share_s": 3, "share_r": 3}
DEEP = 7


def buffers(r, c):
    h = r // 2
    shapes = {"mine": (4, r, c), "partner": (4, r, c), "sums": (3, r, c), "first": (4, h, c), "second": (2, h, c)}
    shapes.update({name: (r, c) for name in ("m", "v", "w", "g", "new")})
    return {name: pltpu.VMEM((RING[name], *shape), jnp.float32 if name in ("m", "v") else jnp.bfloat16) for name, shape in shapes.items()}


def widths(r, columns):
    target = 150_000 // r
    best = 128
    for c in range(128, columns + 1, 128):
        if columns % c == 0 and abs(c - target) < abs(best - target):
            best = c
    return best


def fit(n, *sizes):
    return next(s for s in sizes if n % s == 0)


def contract(a, b, dims):
    return lax.dot_general(a, b, ((dims, dims), ((), ())), preferred_element_type=jnp.float32)


def gradient_piece(a, b, out):
    tokens, rows = a.shape
    columns = b.shape[1]

    def body(a, b, out):
        out[...] = contract(a[...], b[...], (0,)).astype(jnp.bfloat16)

    if rows <= columns:
        tm, tn = rows, fit(columns, 256, 128)
    else:
        tm, tn = fit(rows, 512, 256, 128), columns
    pltpu.emit_pipeline(
        body,
        grid=(rows // tm, columns // tn),
        in_specs=[pl.BlockSpec((tokens, tm), lambda i, j: (0, i)), pl.BlockSpec((tokens, tn), lambda i, j: (0, j))],
        out_specs=[pl.BlockSpec((tm, tn), lambda i, j: (i, j))],
    )(a, b, out)


def hidden_piece(dy, w, gate, up, dgate, dup):
    tokens, d = dy.shape
    ff = w.shape[0]
    tn = fit(ff, 256, 128)

    def body(dy, w, gate, up, dgate, dup):
        dp = contract(dy[...], w[...], (1,)).astype(jnp.bfloat16).astype(jnp.float32)
        dgate[...] = (dp * gate[...]).astype(jnp.bfloat16)
        dup[...] = (dp * up[...]).astype(jnp.bfloat16)

    tile = pl.BlockSpec((tokens, tn), lambda j: (0, j))
    pltpu.emit_pipeline(
        body,
        grid=(ff // tn,),
        in_specs=[pl.BlockSpec((tokens, d), lambda j: (0, 0)), pl.BlockSpec((tn, d), lambda j: (j, 0)), tile, tile],
        out_specs=[tile, tile],
    )(dy, w, gate, up, dgate, dup)


def input_piece(dh, w, out, other=None):
    tokens, ff = dh.shape
    columns = w.shape[0]
    tn = fit(columns, 256, 128)

    def body(dh, w, *rest):
        new = contract(dh[...], w[...], (1,)).astype(jnp.bfloat16)
        rest[-1][...] = rest[0][...] + new if len(rest) > 1 else new

    tile = pl.BlockSpec((tokens, tn), lambda j: (0, j))
    pltpu.emit_pipeline(
        body,
        grid=(columns // tn,),
        in_specs=[pl.BlockSpec((tokens, ff), lambda j: (0, 0)), pl.BlockSpec((tn, ff), lambda j: (j, 0))] + [tile] * (other is not None),
        out_specs=[tile],
    )(dh, w, *([] if other is None else [other]), out)


def norm_piece(h, da, dy, out):
    tokens, d = h.shape
    tm = fit(tokens, 256, 128)

    def body(h, da, dy, out):
        wide, da = h[...].astype(jnp.float32), da[...].astype(jnp.float32)
        scale = lax.rsqrt(jnp.mean(wide**2, -1, keepdims=True) + 1e-6)
        back = da * scale - wide * (scale * scale * scale * jnp.mean(da * wide, -1, keepdims=True))
        out[...] = dy[...] + back.astype(jnp.bfloat16)

    tile = pl.BlockSpec((tm, d), lambda i: (i, 0))
    pltpu.emit_pipeline(body, grid=(tokens // tm,), in_specs=[tile] * 3, out_specs=[tile])(h, da, dy, out)


BUDGET = 20.0


def backward(size, number, n, layers, above, saved, below, given, ws, ms, vs):
    d, ff = ws[0].shape[1:]
    tokens = above.shape[0]
    shapes = [w.shape[1:] for w in ws]
    kinds = sorted(set(shapes))
    width = {k: widths(k[0] // size, k[1]) for k in kinds}
    bf = jnp.bfloat16
    like = jax.ShapeDtypeStruct
    groups = [("above", [above]), ("w", ws), ("m", ms), ("v", vs)] + [(name, [saved[name]]) for name in ("a", "h", "slope", "silu", "p")]
    results = [("new", [like(s, bf) for s in shapes]), ("block", [like((s[0] // size, s[1]), bf) for s in shapes])]
    results += [("grad", [like(s, bf) for s in shapes[:2]])]
    if given is None:
        results += [("given", [like(shapes[2], bf)] + [like((tokens, ff), bf)] * 2)]
    else:
        groups += [("given", given)]
    if below is not None:
        groups += [("b_" + name, [below[name]]) for name in ("slope", "silu", "p")]
        results += [("next", [like(shapes[2], bf)] + [like((tokens, ff), bf)] * 2)]
        results += [(name, [like((tokens, d), bf)]) for name in ("part", "da", "dh")]

    def kernel(*refs):
        at = 0
        ref = {}
        for name, arrays in groups + results:
            ref[name] = refs[at : at + len(arrays)]
            at += len(arrays)
        bufs = {}
        for k in kinds:
            bufs[k] = dict(zip(RING, refs[at : at + len(RING)], strict=True))
            at += len(RING)
        sems = dict(zip(SEMS, refs[at:], strict=True))
        place = Place(size)
        barrier = pltpu.get_barrier_semaphore()
        for to in (place.partner, place.side(0), place.side(1)):
            pl.semaphore_signal(barrier, inc=1, device_id={"dp": to}, device_id_type=MESH)
        pl.semaphore_wait(barrier, 3)

        units, pieces, ready = [], [], []

        def weight(which, grad, a=None, b=None, send=True):
            shape = shapes[which]
            c = width[shape]
            count = shape[1] // c
            for first, last in ((0, (count + 1) // 2), ((count + 1) // 2, count)):
                some = pl.ds(first * c, (last - first) * c)
                if a is not None:
                    cost = 2 * tokens * shape[0] * c * (last - first) / 0.8e9 + 2
                    pieces.append((cost, lambda some=some: gradient_piece(a, b.at[:, some], grad.at[:, some])))
                for i in range(first, last) if send else ():
                    the = (grad, *(ref[x][which] for x in ("w", "m", "v", "new", "block")))
                    units.append(Unit(len(units), place, the, n, pl.ds(i * c, c), bufs[shape], sems))
                    ready.append(len(pieces))

        def hidden(n, above, slope, silu, dgate, dup):
            for start in range(0, tokens, tokens // 2):
                some = pl.ds(start, tokens // 2)
                pieces.append((20, lambda some=some: hidden_piece(
                    above.at[some], ref["w"][2].at[n], *(one.at[some] for one in (slope, silu, dgate, dup)))))

        above, (a,), (h,) = ref["above"][0], ref["a"], ref["h"]
        down, dgate, dup = ref["given"]
        if given is None:
            weight(2, down, ref["p"][0], above)
            hidden(n, above, ref["slope"][0], ref["silu"][0], dgate, dup)
        else:
            weight(2, down)
        weight(0, ref["grad"][0], a, dgate)
        weight(1, ref["grad"][1], a, dup)
        if below is not None:
            (part,), (da,), (dh,) = ref["part"], ref["da"], ref["dh"]
            for start in range(0, tokens, tokens // 2):
                some = pl.ds(start, tokens // 2)
                pieces.append((17, lambda some=some: input_piece(dgate.at[some], ref["w"][0].at[n], part.at[some])))
                pieces.append((17, lambda some=some: input_piece(dup.at[some], ref["w"][1].at[n], da.at[some], part.at[some])))
            pieces.append((9, lambda: norm_piece(h, da, above, dh)))
            weight(2, ref["next"][0], ref["b_p"][0], dh, send=False)
            hidden(n - 1, dh, ref["b_slope"][0], ref["b_silu"][0], *ref["next"][1:])

        done = 0
        for t in range(len(units) + 6):
            if t < len(units):
                while done < ready[t]:
                    pieces[done][1]()
                    done += 1
            for stage in range(6, -1, -1):
                if 0 <= t - stage < len(units):
                    getattr(units[t - stage], f"s{stage}")()
            spent = 0.0
            while done < len(pieces) and spent + pieces[done][0] <= BUDGET:
                spent += pieces[done][0]
                pieces[done][1]()
                done += 1
        while done < len(pieces):
            pieces[done][1]()
            done += 1

    anywhere = pl.BlockSpec(memory_space=pl.ANY)
    scratch = []
    for k in kinds:
        scratch += list(buffers(k[0] // size, width[k]).values())
    scratch += [pltpu.SemaphoreType.DMA((DEEP, count)) for count in SEMS.values()]
    operands = [one for _, arrays in groups for one in arrays]
    outs = [one for _, arrays in results for one in arrays]
    out = pl.pallas_call(
        kernel,
        out_shape=outs,
        in_specs=[anywhere] * len(operands),
        out_specs=[anywhere] * len(outs),
        scratch_shapes=scratch,
        compiler_params=pltpu.CompilerParams(collective_id=number, has_side_effects=True, vmem_limit_bytes=63 * 2**20),
        name=f"backward{number}",
    )(*operands)
    got, at = {}, 0
    for name, arrays in results:
        got[name] = list(out[at : at + len(arrays)])
        at += len(arrays)
    return got


def matmul(a, w):
    return jnp.dot(a, w, preferred_element_type=jnp.float32).astype(jnp.bfloat16)


def normed(h):
    wide = h.astype(jnp.float32)
    scale = lax.rsqrt(jnp.mean(wide**2, -1, keepdims=True) + 1e-6)
    return (wide * scale).astype(jnp.bfloat16)


def solution(mesh):
    size = mesh.shape["dp"]

    def local(x, dy, *arrays):
        ws, ms, vs = (arrays[i : i + 3] for i in (0, 3, 6))
        h, dy = x[0], dy[0]
        layers = ws[0].shape[0]
        saved = []
        for n in range(layers):
            a = normed(h)
            gate = jnp.dot(a, ws[0][n], preferred_element_type=jnp.float32)
            up = jnp.dot(a, ws[1][n], preferred_element_type=jnp.float32)
            share = jax.nn.sigmoid(gate)
            silu = gate * share
            p = (silu * up).astype(jnp.bfloat16)
            slope = up * (share + silu * (1 - share))
            saved.append({"a": a, "h": h, "slope": slope, "silu": silu, "p": p})
            if n < layers - 1:
                h = h + matmul(p, ws[2][n])
        new, blocks, given = [None] * layers, [None] * layers, None
        for number, n in enumerate(reversed(range(layers))):
            got = backward(size, number, n, layers, dy, saved[n], saved[n - 1] if n else None, given, ws, ms, vs)
            new[n], blocks[n] = got["new"], got["block"]
            if n:
                given, dy = got["next"], got["dh"][0]
        new, blocks = ([jnp.stack(one) for one in zip(*all, strict=True)] for all in (new, blocks))
        out_m, out_v = [], []
        for g, m, v in zip(blocks, ms, vs, strict=True):
            g = g.astype(jnp.float32)
            _, m, v = adamw(jnp.zeros_like(g), m, v, g)
            out_m.append(m)
            out_v.append(v)
        return (*new, *out_m, *out_v)

    tokens, whole, rows, groups = P(("rep", "dp"), None, None), P(None, None, None), P(None, "dp", None), P("rep", None, None)
    return jax.shard_map(
        local,
        mesh=mesh,
        in_specs=(tokens,) * 2 + (whole,) * 3 + (rows,) * 6,
        out_specs=(groups,) * 3 + (P("rep", "dp", None),) * 6,
        check_vma=False,
    )
```

time: 1180 us -> 881 us (0.75)
  Pallas kernels: 0 us -> 634 us
  waiting for transfers between devices: 566 us -> 0 us
  matrix products: 427 us -> 162 us
  local copies, waits for them, and re-layouts: 54.9 us -> 0.42 us
  other arithmetic: 107 us -> 71.9 us
  between operations: 15.1 us -> 1.23 us
    pallas_call x0 -> x2, Pallas kernels: none -> 634 us  [backward(): pl.pallas_call(kernel, out_shape=outs, in_specs=[anywhere] * len(operands...]
    unnamed x15 -> x0, waiting for transfers between devices: 305 us -> none
    reshape x3 -> x0, waiting for transfers between devices: 261 us -> none  [step(): t.reshape(-1, *t.shape[2:])]
    dot_general x10 -> x4, matrix products: 291 us -> 136 us  [the longest x2 84.4 us: local(): up = jnp.dot(a, ws[1][n], preferred_element_type=jnp.float32)]
    dot_general x5 -> x1, matrix products: 136 us -> 26.3 us  [matmul(): jnp.dot(a, w, preferred_element_type=jnp.float32).astype(jnp.bfloat16)]
    unnamed x6 -> x2, other arithmetic: 68.3 us -> 0.01 us
    unnamed x41 -> x28, local copies, waits for them, and re-layouts: 54.3 us -> 0.42 us
    another operation x0 -> x2, other arithmetic: none -> 35.7 us  [local(): jnp.stack(one)]
  transfers between devices with their start and end apart: 9 -> 0, of which waited for: 7 -> 0; matrix products, arithmetic and copies ran while one was open for 30% -> 0% of each run, Pallas kernels for 0% -> 0%
where the time goes in v1:
time: 881 us; the launch traced here: 869 us
  Pallas kernels  634 us (72%)
  matrix products  162 us (18%)
  other arithmetic  71.9 us (8%)
    pallas_call x2, Pallas kernels, backward(): pl.pallas_call(kernel, out_shape=outs, in_specs=[anywhere] * len(operands...  634 us
    dot_general x2, matrix products, local(): up = jnp.dot(a, ws[1][n], preferred_element_type=jnp.float32)  84.4 us
    dot_general x2, matrix products, local(): gate = jnp.dot(a, ws[0][n], preferred_element_type=jnp.float32)  51.2 us
    another operation x2, other arithmetic, local(): jnp.stack(one)  35.7 us
    dot_general x1, matrix products, matmul(): jnp.dot(a, w, preferred_element_type=jnp.float32).astype(jnp.bfloat16)  26.3 us
    add x2, other arithmetic, adamw(): v = 0.95 * v + 0.05 * g * g  21.2 us

profile of v1, /device:TPU:113, one launch (start us, length us, event | category | flops | bytes accessed | tf_op | source)
XLA Modules:
  0.0 869.5 jit_solution(6046377255537255241)
XLA Ops:
  0.6 3.6 fusion.2
  4.2 0.0 copy-start.4
  4.2 27.1 %fusion.14 = f32[2048,3584]{1,0:T(8,128)} fusion(bf16[2,1280,3584]{2,1,0:T(8,128)(2,1)} %refs_1_.3, bf16[1,2048,1280]{2,1,0:T(8,128)(2,1)} %param.11, f32[2048]{0:T(1024)S(1)} %add_rsqrt_fusion.1), kind=kOutput, calls=%fused_computation.28 | convolution fusion | flops 18798346240 | bytes 43786240 | tf_op jit(solution)/shard_map/dot_general | solution.py:444
  31.4 42.0 %add_multiply_fusion = (f32[2048,3584]{1,0:T(8,128)}, bf16[2048,3584]{1,0:T(8,128)(2,1)}, f32[2048,3584]{1,0:T(8,128)}) fusion(f32[2048,3584]{1,0:T(8,128)} %fusion.14, bf16[2,1280,3584]{2,1,0:T(8,128)(2,1)} %refs_2_.3, bf16[1,2048,1280]{2,1,0:T(8,128)(2,1)} %param.11, f32[2048]{0:T(1024)S(1)} %add_rsqrt_fusion.1), kind=kOutput, calls=%fused_computation | convolution fusion | flops 18871746560 | bytes 117186560 | tf_op jit(solution)/shard_map/dot_general | solution.py:445
  73.3 0.0 slice-start.2
  73.3 0.0 slice-start.3
  73.3 0.0 slice-start.4
  73.4 26.3 %fusion.4 = (f32[2048]{0:T(1024)S(1)}, bf16[2048,1280]{1,0:T(8,128)(2,1)}) fusion(bf16[2048,3584]{1,0:T(8,128)(2,1)} %get-tuple-element.42.refs_17_.refs_14_, bf16[2,3584,1280]{2,1,0:T(8,128)(2,1)} %refs_3_.3, bf16[1,2048,1280]{2,1,0:T(8,128)(2,1)} %param.11), kind=kOutput, calls=%fused_computation.17 | convolution fusion | flops 18803587072 | bytes 34349056 | tf_op jit(solution)/shard_map/dot_general | solution.py:425
  99.7 5.7 fusion.5.refs_10_
  105.4 0.0 slice-done.3
  105.4 0.0 slice-done.4
  105.4 24.1 %fusion.6 = f32[2048,3584]{1,0:T(8,128)} fusion(bf16[2048,1280]{1,0:T(8,128)(2,1)} %fusion.5.refs_10_, bf16[2,1280,3584]{2,1,0:T(8,128)(2,1)S(1)} %bitcast.52), kind=kOutput, calls=%fused_computation.20 | convolution fusion | flops 18790481920 | bytes 43778048 | tf_op jit(solution)/shard_map/dot_general | solution.py:444
  129.5 42.4 %multiply_convert_fusion = (bf16[2048,3584]{1,0:T(8,128)(2,1)}, f32[2048,3584]{1,0:T(8,128)}, f32[2048,3584]{1,0:T(8,128)}) fusion(f32[2048,3584]{1,0:T(8,128)} %fusion.6, bf16[2048,1280]{1,0:T(8,128)(2,1)} %fusion.5.refs_10_, bf16[2,1280,3584]{2,1,0:T(8,128)(2,1)} %refs_2_.3), kind=kOutput, calls=%fused_computation.1 | convolution fusion | flops 18863882240 | bytes 117178368 | tf_op jit(solution)/shard_map/dot_general | solution.py:445
  171.9 359.7 %backward0.1 = (bf16[1280,3584]{1,0:T(8,128)(2,1)}, bf16[1280,3584]{1,0:T(8,128)(2,1)}, bf16[3584,1280]{1,0:T(8,128)(2,1)}, bf16[160,3584]{1,0:T(8,128)(2,1)}, b...) custom-call(bf16[2048,1280]{1,0:T(8,128)(2,1)} %bitcast.62, ...), custom_call_target="tpu_custom_call" | custom-call | tf_op jit(solution)/shard_map/backward0/pallas_call | solution.py:408
  531.6 5.8 fusion.3.refs_10_
  537.4 274.3 %backward1.1 = (bf16[1280,3584]{1,0:T(8,128)(2,1)}, bf16[1280,3584]{1,0:T(8,128)(2,1)}, bf16[3584,1280]{1,0:T(8,128)(2,1)}, bf16[160,3584]{1,0:T(8,128)(2,1)}, b...) custom-call(bf16[2048,1280]{1,0:T(8,128)(2,1)} %get-tuple-element.25, ...), custom_call_target="tpu_custom_call" | custom-call | tf_op jit(solution)/shard_map/backward1/pallas_call | solution.py:408
  811.7 0.0 copy-start
  811.7 0.0 copy-start.1
  811.7 0.0 slice-start.5
  811.7 8.0 fusion.33
  819.8 0.4 copy-done.3
  820.1 13.2 %fusion.31 = (f32[2,160,3584]{2,1,0:T(8,128)}, f32[2,160,3584]{2,1,0:T(8,128)}, f32[2,160,3584]{2,1,0:T(8,128)}, f32[2,160,3584]{2,1,0:T(8,128)}) fusion(f32[2,160,3584]{2,1,0:T(8,128)} %refs_7_.3, bf16[1,160,3584]{2,1,0:T(8,128)(2,1)S(1)} %bitcast.63, bf16[1,160,3584]{2,1,0:T(8,128)(2,1)S(1)} %bitcast.66, f32[2,160,3584]{2,1,0:T(8,128)} %refs_4_.3, ...), kind=kLoop, calls=%fused_computation.47 | loop fusion | flops 20643840 | bytes 41287680 | tf_op jit(solution)/shard_map/add | solution.py:14
  833.4 11.5 %pad_maximum_fusion.2 = bf16[2,3584,1280]{2,1,0:T(8,128)(2,1)} fusion(bf16[1,3584,1280]{2,1,0:T(8,128)(2,1)S(1)} %bitcast.60, bf16[1,3584,1280]{2,1,0:T(8,128)(2,1)} %bitcast.61), kind=kLoop, calls=%fused_computation.10 | loop fusion | flops 9175040 | bytes 36700160 | tf_op jit(solution)/shard_map/stack | solution.py:459
  844.9 24.2 %pad_maximum_fusion = (bf16[2,1280,3584]{2,1,0:T(8,128)(2,1)}, bf16[2,1280,3584]{2,1,0:T(8,128)(2,1)}) fusion(bf16[1,1280,3584]{2,1,0:T(8,128)(2,1)} %bitcast.54, bf16[1,1280,3584]{2,1,0:T(8,128)(2,1)} %bitcast.56, bf16[1,1280,3584]{2,1,0:T(8,128)(2,1)} %bitcast.55, bf16[1,1280,3584]{2,1,0:T(8,128)(2,1)} %bitcast.57), kind=kLoop, calls=%fused_computation.8 | loop fusion | flops 18350080 | bytes 73400320 | tf_op jit(solution)/shard_map/stack | solution.py:459
  (22 shorter events, 0.1 us)
Async XLA Ops:
  4.2 27.1 %copy-start.4 = (f32[2048]{0:T(1024)}, f32[2048]{0:T(1024)S(1)}, u32[]{:S(2)}) copy-start(f32[2048]{0:T(1024)S(1)} %add_rsqrt_fusion.1) | copy-start | bytes 24580
  73.3 32.1 %slice-start = ((s8[18350080]{0:T(1024)(128)(4,1)}), s8[4194304]{0:T(1024)(128)(4,1)S(1)}, s32[]{:S(2)}) async-start(s8[18350080]{0:T(1024)(128)(4,1)} %bitcast.51), calls=%async_computation | async-start | bytes 8388608
  73.3 32.1 %slice-start.1 = ((s8[18350080]{0:T(1024)(128)(4,1)}), s8[4194304]{0:T(1024)(128)(4,1)S(1)}, s32[]{:S(2)}) async-start(s8[18350080]{0:T(1024)(128)(4,1)} %bitcast.51), calls=%async_computation.1 | async-start | bytes 8388608
  73.3 32.1 %slice-start.2 = ((s8[18350080]{0:T(1024)(128)(4,1)}), s8[4194304]{0:T(1024)(128)(4,1)S(1)}, s32[]{:S(2)}) async-start(s8[18350080]{0:T(1024)(128)(4,1)} %bitcast.51), calls=%async_computation.2 | async-start | bytes 8388608
  73.3 32.1 %slice-start.3 = ((s8[18350080]{0:T(1024)(128)(4,1)}), s8[4194304]{0:T(1024)(128)(4,1)S(1)}, s32[]{:S(2)}) async-start(s8[18350080]{0:T(1024)(128)(4,1)} %bitcast.51), calls=%async_computation.3 | async-start | bytes 8388608
  73.3 32.1 %slice-start.4 = ((s8[18350080]{0:T(1024)(128)(4,1)}), s8[1572864]{0:T(1024)(128)(4,1)S(1)}, s32[]{:S(2)}) async-start(s8[18350080]{0:T(1024)(128)(4,1)} %bitcast.51), calls=%async_computation.4 | async-start | bytes 3145728
  171.9 359.7 %copy-start.5 = (f32[2048]{0:T(1024)S(1)}, f32[2048]{0:T(1024)}, u32[]{:S(2)}) copy-start(f32[2048]{0:T(1024)} %copy-done.4) | copy-start | bytes 24580
  811.7 8.1 copy-start
  811.7 8.1 copy-start.1
  811.7 8.1 copy-start.2
  811.7 8.4 copy-start.3
  811.7 21.6 %slice-start.5 = ((s8[9175040]{0:T(1024)(128)(4,1)}), s8[4194304]{0:T(1024)(128)(4,1)S(1)}, s32[]{:S(2)}) async-start(s8[9175040]{0:T(1024)(128)(4,1)} %bitcast.58), calls=%async_computation.5 | async-start | bytes 8388608
  819.8 13.6 %slice-start.6 = ((s8[9175040]{0:T(1024)(128)(4,1)}), s8[4194304]{0:T(1024)(128)(4,1)S(1)}, s32[]{:S(2)}) async-start(s8[9175040]{0:T(1024)(128)(4,1)} %bitcast.58), calls=%async_computation.6 | async-start | bytes 8388608
  820.1 13.2 %slice-start.7 = ((s8[9175040]{0:T(1024)(128)(4,1)}), s8[786432]{0:T(1024)(128)(4,1)S(1)}, s32[]{:S(2)}) async-start(s8[9175040]{0:T(1024)(128)(4,1)} %bitcast.58), calls=%async_computation.7 | async-start | bytes 1572864

commit v2 on v1

--- a/solution.py
+++ b/solution.py
@@ -317,9 +317,10 @@
         results += [("given", [like(shapes[2], bf)] + [like((tokens, ff), bf)] * 2)]
     else:
         groups += [("given", given)]
+        results += [("hidden", [like((tokens, ff), bf)] * 2)]
     if below is not None:
-        groups += [("b_" + name, [below[name]]) for name in ("slope", "silu", "p")]
-        results += [("next", [like(shapes[2], bf)] + [like((tokens, ff), bf)] * 2)]
+        groups += [("b_p", [below["p"]])]
+        results += [("next", [like(shapes[2], bf)])]
         results += [(name, [like((tokens, d), bf)]) for name in ("part", "da", "dh")]
 
     def kernel(*refs):
@@ -362,12 +363,13 @@
                     above.at[some], ref["w"][2].at[n], *(one.at[some] for one in (slope, silu, dgate, dup)))))
 
         above, (a,), (h,) = ref["above"][0], ref["a"], ref["h"]
-        down, dgate, dup = ref["given"]
         if given is None:
+            down, dgate, dup = ref["given"]
             weight(2, down, ref["p"][0], above)
-            hidden(n, above, ref["slope"][0], ref["silu"][0], dgate, dup)
         else:
+            (down,), (dgate, dup) = ref["given"], ref["hidden"]
             weight(2, down)
+        hidden(n, above, ref["slope"][0], ref["silu"][0], dgate, dup)
         weight(0, ref["grad"][0], a, dgate)
         weight(1, ref["grad"][1], a, dup)
         if below is not None:
@@ -378,7 +380,6 @@
                 pieces.append((17, lambda some=some: input_piece(dup.at[some], ref["w"][1].at[n], da.at[some], part.at[some])))
             pieces.append((9, lambda: norm_piece(h, da, above, dh)))
             weight(2, ref["next"][0], ref["b_p"][0], dh, send=False)
-            hidden(n - 1, dh, ref["b_slope"][0], ref["b_silu"][0], *ref["next"][1:])
 
         done = 0
         for t in range(len(units) + 6):

time: 881 us -> 878 us (level)
  no operation moved by 1% of the time
where the time goes in v2:
time: 878 us; the launch traced here: 867 us
  Pallas kernels  631 us (72%)
  matrix products  162 us (18%)
  other arithmetic  71.9 us (8%)
    pallas_call x2, Pallas kernels, backward(): pl.pallas_call(kernel, out_shape=outs, in_specs=[anywhere] * len(operands...  631 us
    dot_general x2, matrix products, local(): up = jnp.dot(a, ws[1][n], preferred_element_type=jnp.float32)  84.4 us
    dot_general x2, matrix products, local(): gate = jnp.dot(a, ws[0][n], preferred_element_type=jnp.float32)  51.2 us
    another operation x2, other arithmetic, local(): jnp.stack(one)  35.7 us
    dot_general x1, matrix products, matmul(): jnp.dot(a, w, preferred_element_type=jnp.float32).astype(jnp.bfloat16)  26.3 us
    add x2, other arithmetic, adamw(): v = 0.95 * v + 0.05 * g * g  21.2 us

profile of v2, /device:TPU:113, one launch (start us, length us, event | category | flops | bytes accessed | tf_op | source)
XLA Modules:
  0.0 866.8 jit_solution(6484717395042995197)
XLA Ops:
  0.6 3.6 fusion.2
  4.2 0.0 copy-start.4
  4.2 27.1 %fusion.14 = f32[2048,3584]{1,0:T(8,128)} fusion(bf16[2,1280,3584]{2,1,0:T(8,128)(2,1)} %refs_1_.3, bf16[1,2048,1280]{2,1,0:T(8,128)(2,1)} %param.11, f32[2048]{0:T(1024)S(1)} %add_rsqrt_fusion.1), kind=kOutput, calls=%fused_computation.28 | convolution fusion | flops 18798346240 | bytes 43786240 | tf_op jit(solution)/shard_map/dot_general | solution.py:445
  31.4 42.0 %add_multiply_fusion = (f32[2048,3584]{1,0:T(8,128)}, bf16[2048,3584]{1,0:T(8,128)(2,1)}, f32[2048,3584]{1,0:T(8,128)}) fusion(f32[2048,3584]{1,0:T(8,128)} %fusion.14, bf16[2,1280,3584]{2,1,0:T(8,128)(2,1)} %refs_2_.3, bf16[1,2048,1280]{2,1,0:T(8,128)(2,1)} %param.11, f32[2048]{0:T(1024)S(1)} %add_rsqrt_fusion.1), kind=kOutput, calls=%fused_computation | convolution fusion | flops 18871746560 | bytes 117186560 | tf_op jit(solution)/shard_map/dot_general | solution.py:446
  73.3 0.0 slice-start.2
  73.3 0.0 slice-start.3
  73.3 0.0 slice-start.4
  73.4 26.3 %fusion.4 = (f32[2048]{0:T(1024)S(1)}, bf16[2048,1280]{1,0:T(8,128)(2,1)}) fusion(bf16[2048,3584]{1,0:T(8,128)(2,1)} %get-tuple-element.38.refs_15_.refs_14_, bf16[2,3584,1280]{2,1,0:T(8,128)(2,1)} %refs_3_.3, bf16[1,2048,1280]{2,1,0:T(8,128)(2,1)} %param.11), kind=kOutput, calls=%fused_computation.17 | convolution fusion | flops 18803587072 | bytes 34349056 | tf_op jit(solution)/shard_map/dot_general | solution.py:426
  99.7 5.7 fusion.5.refs_10_
  105.4 0.0 slice-done.3
  105.4 0.0 slice-done.4
  105.4 24.1 %fusion.6 = f32[2048,3584]{1,0:T(8,128)} fusion(bf16[2048,1280]{1,0:T(8,128)(2,1)} %fusion.5.refs_10_, bf16[2,1280,3584]{2,1,0:T(8,128)(2,1)S(1)} %bitcast.52), kind=kOutput, calls=%fused_computation.20 | convolution fusion | flops 18790481920 | bytes 43778048 | tf_op jit(solution)/shard_map/dot_general | solution.py:445
  129.5 42.4 %multiply_convert_fusion = (bf16[2048,3584]{1,0:T(8,128)(2,1)}, f32[2048,3584]{1,0:T(8,128)}, f32[2048,3584]{1,0:T(8,128)}) fusion(f32[2048,3584]{1,0:T(8,128)} %fusion.6, bf16[2048,1280]{1,0:T(8,128)(2,1)} %fusion.5.refs_10_, bf16[2,1280,3584]{2,1,0:T(8,128)(2,1)} %refs_2_.3), kind=kOutput, calls=%fused_computation.1 | convolution fusion | flops 18863882240 | bytes 117178368 | tf_op jit(solution)/shard_map/dot_general | solution.py:446
  171.9 327.7 %backward0.1 = (bf16[1280,3584]{1,0:T(8,128)(2,1)}, bf16[1280,3584]{1,0:T(8,128)(2,1)}, bf16[3584,1280]{1,0:T(8,128)(2,1)}, bf16[160,3584]{1,0:T(8,128)(2,1)}, b...) custom-call(bf16[2048,1280]{1,0:T(8,128)(2,1)} %bitcast.62, ...), custom_call_target="tpu_custom_call" | custom-call | tf_op jit(solution)/shard_map/backward0/pallas_call | solution.py:409
  499.6 5.8 fusion.3.refs_10_
  505.3 303.7 %backward1.1 = (bf16[1280,3584]{1,0:T(8,128)(2,1)}, bf16[1280,3584]{1,0:T(8,128)(2,1)}, bf16[3584,1280]{1,0:T(8,128)(2,1)}, bf16[160,3584]{1,0:T(8,128)(2,1)}, b...) custom-call(bf16[2048,1280]{1,0:T(8,128)(2,1)} %get-tuple-element.23, ...), custom_call_target="tpu_custom_call" | custom-call | tf_op jit(solution)/shard_map/backward1/pallas_call | solution.py:409
  809.1 0.0 slice-start.5
  809.1 8.0 fusion.33
  817.1 0.0 copy-done
  817.1 0.0 copy-done.1
  817.1 0.4 copy-done.3
  817.5 13.2 %fusion.31 = (f32[2,160,3584]{2,1,0:T(8,128)}, f32[2,160,3584]{2,1,0:T(8,128)}, f32[2,160,3584]{2,1,0:T(8,128)}, f32[2,160,3584]{2,1,0:T(8,128)}) fusion(f32[2,160,3584]{2,1,0:T(8,128)} %refs_7_.3, bf16[1,160,3584]{2,1,0:T(8,128)(2,1)S(1)} %bitcast.63, bf16[1,160,3584]{2,1,0:T(8,128)(2,1)S(1)} %bitcast.66, f32[2,160,3584]{2,1,0:T(8,128)} %refs_4_.3, ...), kind=kLoop, calls=%fused_computation.47 | loop fusion | flops 20643840 | bytes 41287680 | tf_op jit(solution)/shard_map/add | solution.py:14
  830.7 11.5 %pad_maximum_fusion.2 = bf16[2,3584,1280]{2,1,0:T(8,128)(2,1)} fusion(bf16[1,3584,1280]{2,1,0:T(8,128)(2,1)S(1)} %bitcast.60, bf16[1,3584,1280]{2,1,0:T(8,128)(2,1)} %bitcast.61), kind=kLoop, calls=%fused_computation.10 | loop fusion | flops 9175040 | bytes 36700160 | tf_op jit(solution)/shard_map/stack | solution.py:460
  842.2 24.2 %pad_maximum_fusion = (bf16[2,1280,3584]{2,1,0:T(8,128)(2,1)}, bf16[2,1280,3584]{2,1,0:T(8,128)(2,1)}) fusion(bf16[1,1280,3584]{2,1,0:T(8,128)(2,1)} %bitcast.54, bf16[1,1280,3584]{2,1,0:T(8,128)(2,1)} %bitcast.56, bf16[1,1280,3584]{2,1,0:T(8,128)(2,1)} %bitcast.55, bf16[1,1280,3584]{2,1,0:T(8,128)(2,1)} %bitcast.57), kind=kLoop, calls=%fused_computation.8 | loop fusion | flops 18350080 | bytes 73400320 | tf_op jit(solution)/shard_map/stack | solution.py:460
  (22 shorter events, 0.1 us)
Async XLA Ops:
  4.2 27.1 %copy-start.4 = (f32[2048]{0:T(1024)}, f32[2048]{0:T(1024)S(1)}, u32[]{:S(2)}) copy-start(f32[2048]{0:T(1024)S(1)} %add_rsqrt_fusion.1) | copy-start | bytes 24580
  73.3 32.0 %slice-start = ((s8[18350080]{0:T(1024)(128)(4,1)}), s8[4194304]{0:T(1024)(128)(4,1)S(1)}, s32[]{:S(2)}) async-start(s8[18350080]{0:T(1024)(128)(4,1)} %bitcast.51), calls=%async_computation | async-start | bytes 8388608
  73.3 32.0 %slice-start.1 = ((s8[18350080]{0:T(1024)(128)(4,1)}), s8[4194304]{0:T(1024)(128)(4,1)S(1)}, s32[]{:S(2)}) async-start(s8[18350080]{0:T(1024)(128)(4,1)} %bitcast.51), calls=%async_computation.1 | async-start | bytes 8388608
  73.3 32.0 %slice-start.2 = ((s8[18350080]{0:T(1024)(128)(4,1)}), s8[4194304]{0:T(1024)(128)(4,1)S(1)}, s32[]{:S(2)}) async-start(s8[18350080]{0:T(1024)(128)(4,1)} %bitcast.51), calls=%async_computation.2 | async-start | bytes 8388608
  73.3 32.0 %slice-start.3 = ((s8[18350080]{0:T(1024)(128)(4,1)}), s8[4194304]{0:T(1024)(128)(4,1)S(1)}, s32[]{:S(2)}) async-start(s8[18350080]{0:T(1024)(128)(4,1)} %bitcast.51), calls=%async_computation.3 | async-start | bytes 8388608
  73.3 32.0 %slice-start.4 = ((s8[18350080]{0:T(1024)(128)(4,1)}), s8[1572864]{0:T(1024)(128)(4,1)S(1)}, s32[]{:S(2)}) async-start(s8[18350080]{0:T(1024)(128)(4,1)} %bitcast.51), calls=%async_computation.4 | async-start | bytes 3145728
  171.9 327.7 %copy-start.5 = (f32[2048]{0:T(1024)S(1)}, f32[2048]{0:T(1024)}, u32[]{:S(2)}) copy-start(f32[2048]{0:T(1024)} %copy-done.4) | copy-start | bytes 24580
  809.0 8.1 copy-start
  809.0 8.1 copy-start.1
  809.0 8.1 copy-start.2
  809.1 8.4 copy-start.3
  809.1 21.6 %slice-start.5 = ((s8[9175040]{0:T(1024)(128)(4,1)}), s8[4194304]{0:T(1024)(128)(4,1)S(1)}, s32[]{:S(2)}) async-start(s8[9175040]{0:T(1024)(128)(4,1)} %bitcast.58), calls=%async_computation.5 | async-start | bytes 8388608
  817.1 13.6 %slice-start.6 = ((s8[9175040]{0:T(1024)(128)(4,1)}), s8[4194304]{0:T(1024)(128)(4,1)S(1)}, s32[]{:S(2)}) async-start(s8[9175040]{0:T(1024)(128)(4,1)} %bitcast.58), calls=%async_computation.6 | async-start | bytes 8388608
  817.5 13.2 %slice-start.7 = ((s8[9175040]{0:T(1024)(128)(4,1)}), s8[786432]{0:T(1024)(128)(4,1)S(1)}, s32[]{:S(2)}) async-start(s8[9175040]{0:T(1024)(128)(4,1)} %bitcast.58), calls=%async_computation.7 | async-start | bytes 1572864
